TPU v7x, 32 devices: a whole 2x2x4 slice. The times are simulated.
32 devices in a mesh: gx: 8 (over y, x, core), gy: 4 (over z).
Axes of the slice: x: 2, y: 2, z: 4, core: 2. Of those that a mesh axis runs over, the one named last changes fastest.
Arguments:
- date_key: int32 [393216], P(('gx', 'gy')), may hold values from 0 to 4095
- store_key: int32 [393216], P(('gx', 'gy')), may hold values from 0 to 65535
- product_key: int32 [393216], P(('gx', 'gy')), may hold values from 0 to 1048575
- revenue: bfloat16 [393216], P(('gx', 'gy')), may hold values from -0.59765625 to 0.59765625
- row_counts: int32 [32], P(('gx', 'gy')), may hold values from 1 to 12288, 245760 in all
- date_years: int32 [512], P('gx'), may hold values from -2147483648 to 2147483646
- date_flags: int32 [128], P('gx'), may hold values from -2147483648 to 2147483646
- store_flags: int32 [2048], P('gx'), may hold values from -2147483648 to 2147483646
- product_flags: int32 [32768], P('gx'), may hold values from -2147483648 to 2147483646
- brand_words: int32 [349568], P('gx'), may hold values from 0 to 1073741823
Outputs:
- revenue_groups: float32 [16, 1024], replicated
Inputs may be any that keep to these rules, and one draw needn't show every extreme that they name: Rows d * 12288 to d * 12288 + row_counts[d] - 1 of the fact arrays are live; the largest count equals 12288. `date_years`: date k's year code is in bits 4 * (k % 8) of word k // 8. `date_flags`: bit k % 32 of word k // 32 is the flag of row k. `store_flags`: bit k % 32 of word k // 32 is the flag of row k. `product_flags`: bit k % 32 of word k // 32 is the flag of row k. `brand_words`: product with shard o and local index l holds its brand code in bits 10 * (l % 3) of word o * 43696 + l // 3; words past a shard's products are unused.
All inputs are finite; a program needn't handle non-finite values. No bound on the sum of `row_counts` on one device may be relied on, other than what follows from the above.
Results may differ from a plain program's by a relative error of at most 0.0003.
Values sent between devices are 32-bit elements; how exact they have to be, the bound alone decides.
A program may use at most 64 MiB of HBM per device.

v0:
```python
import jax
import jax.numpy as jnp
from jax import lax
from jax.sharding import PartitionSpec as P

BRANDS = 1024
YEARS = 16


def pick_bits(packed, position, width_bits):
    per_word = 32 // width_bits
    chosen = packed[position // per_word]
    shifted = jnp.right_shift(chosen, position % per_word * width_bits)
    return jnp.bitwise_and(shifted, (1 << width_bits) - 1)


def shards(
    date_key,
    store_key,
    product_key,
    revenue,
    row_counts,
    date_years,
    date_flags,
    store_flags,
    product_flags,
    brand_words,
):
    flag_shard = product_flags.shape[0]
    brand_shard = brand_words.shape[0]
    prod_shard = flag_shard * 32
    year_words, date_bits, store_bits, product_bits, brand_table = (
        lax.all_gather(date_years, "gx", axis=0, tiled=True),
        lax.all_gather(date_flags, "gx", axis=0, tiled=True),
        lax.all_gather(store_flags, "gx", axis=0, tiled=True),
        lax.all_gather(product_flags, "gx", axis=0, tiled=True),
        lax.all_gather(brand_words, "gx", axis=0, tiled=True),
    )

    def brand_place(owner_idx, word_idx):
        return owner_idx * brand_shard + word_idx

    def flag_place(owner_idx, word_idx):
        return owner_idx * flag_shard + word_idx

    block_rows = min(4096, date_key.shape[0])
    row_count = row_counts[0]
    block_total = (row_count + block_rows - 1) // block_rows
    high_groups = YEARS * BRANDS // 128

    def add_block(block_idx, totals):
        first_row = block_idx * block_rows
        date_block = lax.dynamic_slice_in_dim(date_key, first_row, block_rows, 0)
        store_block = lax.dynamic_slice_in_dim(store_key, first_row, block_rows, 0)
        product_block = lax.dynamic_slice_in_dim(product_key, first_row, block_rows, 0)
        money_block = lax.dynamic_slice_in_dim(revenue, first_row, block_rows, 0)
        live_rows = first_row + lax.iota(jnp.int32, block_rows) < row_count
        year_code = pick_bits(year_words, date_block, 4)
        owner_idx = product_block // prod_shard
        local_idx = product_block % prod_shard
        flag_word = product_bits[flag_place(owner_idx, local_idx // 32)]
        product_pass = jnp.bitwise_and(jnp.right_shift(flag_word, local_idx % 32), 1)
        passed = (
            pick_bits(date_bits, date_block, 1)
            * pick_bits(store_bits, store_block, 1)
            * product_pass
        )
        word_val = brand_table[brand_place(owner_idx, local_idx // 3)]
        brand_code = jnp.bitwise_and(jnp.right_shift(word_val, local_idx % 3 * 10), 1023)
        kept_rows = live_rows & (passed == 1)
        amount = jnp.where(kept_rows, money_block, jnp.zeros_like(money_block))
        high_row = year_code * (BRANDS // 128) + brand_code // 128
        weighted = jnp.where(
            lax.iota(jnp.int32, high_groups)[:, None] == high_row[None, :],
            amount[None, :],
            jnp.zeros((), jnp.bfloat16),
        )
        low_hot = (lax.iota(jnp.int32, 128)[:, None] == (brand_code % 128)[None, :]).astype(
            jnp.bfloat16
        )
        return totals + lax.dot_general(
            weighted, low_hot, (((1,), (1,)), ((), ())), preferred_element_type=jnp.float32
        )

    totals = lax.fori_loop(0, block_total, add_block, jnp.zeros((high_groups, 128), jnp.float32))
    group_sums = totals.reshape(YEARS, BRANDS)
    result = lax.psum(group_sums, ("gx", "gy"))
    return result


def solution(mesh):
    placed = (
        P(("gx", "gy")),
        P(("gx", "gy")),
        P(("gx", "gy")),
        P(("gx", "gy")),
        P(("gx", "gy")),
        P("gx"),
        P("gx"),
        P("gx"),
        P("gx"),
        P("gx"),
    )
    return jax.shard_map(shards, mesh=mesh, in_specs=placed, out_specs=P(), check_vma=False)
```

profile of v0, /device:TPU:1, one launch (start us, length us, event | category | flops | bytes accessed | tf_op | source)
XLA Modules:
  0.0 643.7 jit_solution(12886607325947073091)
XLA Ops:
  6.5 1.3 dynamic-slice
  8.5 0.0 copy-start.7
  8.5 0.0 copy-start.8
  8.5 0.0 copy-start.6
  8.5 0.0 copy-start.5
  8.5 0.0 copy-start.1
  8.5 0.0 copy-start.2
  8.5 0.0 copy-start.3
  8.5 0.1 broadcast.223
  8.6 1.3 dynamic-update-slice.1
  9.9 1.1 copy-done
  11.0 0.0 all-reduce.9.cloned.1.call-update
  11.0 0.0 all-reduce.7.cloned.1.call-start
  13.0 0.2 dynamic-update-slice
  13.3 0.2 dynamic-update-slice.2
  13.5 7.3 %all-reduce.3 = (s32[512]{0:T(512)S(1)}, s32[128]{0:T(128)S(1)}) all-reduce(s32[512]{0:T(512)S(1)} %dynamic-update-slice, s32[128]{0:T(128)S(1)} %dynamic-update-slice.2), channel_id=1, replica_groups=mesh['gx'=8,'gy'=4] {'gx'}, use_global_device_ids=true, to_apply=%add | all-reduce | flops 640 | bytes 5120
  20.8 10.3 %all-gather = s32[8,1,256]{2,1,0:T(1,128)S(1)} all-gather(s32[1,1,256]{2,1,0:T(1,128)S(1)} %bitcast.8), channel_id=1, replica_groups=mesh['gx'=8,'gy'=4] {'gx'}, dimensions={0}, use_global_device_ids=true | all-gather | bytes 9216 | tf_op jit(solution)/shard_map/all_gather | solution.py:35
  31.1 9.0 %all_gather.19 = s32[32768]{0:T(1024)S(1)} all-gather(s32[4096]{0:T(1024)S(1)} %copy-done.5), channel_id=1, replica_groups=mesh['gx'=8,'gy'=4] {'gx'}, dimensions={0}, use_global_device_ids=true | all-gather | bytes 147456 | tf_op jit(solution)/shard_map/all_gather | solution.py:36
  40.1 30.7 %all-reduce.9.cloned.1.call-done = s32[349568]{0:T(1024)} async-done(((s32[349568]{0:T(1024)}), s32[349568]{0:T(1024)}) %all-reduce.9.cloned.1.call-update) | async-done | bytes 1398288
  70.8 147.5 %while.13 = (s32[]{:T(128)}, f32[128,128]{1,0:T(8,128)S(1)}, s32[]{:T(128)}, s32[12288]{0:T(1024)S(1)}, s32[512]{0:T(512)S(1)}, /*index=5*/s32[12288]{0:T(1024)S...) while((s32[]{:T(128)}, f32[128,128]{1,0:T(8,128)S(1)}, ...), condition=%wide.region_1.2_spmd, body=%wide.region_0.1_spmd.sunk | while | flops 136749056 | bytes 860395 | solution.py:85
  70.9 48.5 %gather_fusion.1 = s32[4096]{0:T(1024)S(1)} fusion(s32[349568]{0:T(1024)} %get-tuple-element.421, s32[4096]{0:T(1024)S(1)} %fusion.57), kind=kCustom, calls=%fused_computation.1.clone.1 | custom fusion | bytes 49152 | tf_op jit(solution)/shard_map/while/body/gather | solution.py:68
  119.5 25.9 %gather_fusion = s32[4096]{0:T(1024)S(1)} fusion(s32[512]{0:T(512)S(1)} %get-tuple-element.419, s32[4096]{0:T(1024)S(1)} %fusion.55), kind=kCustom, calls=%fused_computation.clone.1 | custom fusion | bytes 49152 | tf_op jit(solution)/shard_map/while/body/gather | solution.py:12
  145.4 0.1 fusion.58
  145.5 23.0 %gather_fusion.3 = s32[4096]{0:T(1024)S(1)} fusion(s32[2048]{0:T(1024)S(1)} %get-tuple-element.425, s32[4096]{0:T(1024)S(1)} %get-tuple-element.378), kind=kCustom, calls=%fused_computation.3.clone.1 | custom fusion | bytes 49152 | tf_op jit(solution)/shard_map/while/body/gather | solution.py:12
  168.5 23.0 %gather_fusion.2 = s32[4096]{0:T(1024)S(1)} fusion(s32[32768]{0:T(1024)S(1)} %get-tuple-element.426, s32[4096]{0:T(1024)S(1)} %get-tuple-element.377), kind=kCustom, calls=%fused_computation.4.clone.1 | custom fusion | bytes 49152 | tf_op jit(solution)/shard_map/while/body/gather | solution.py:61
  191.6 24.7 %gather_fusion.4 = s32[4096]{0:T(1024)S(1)} fusion(s32[128]{0:T(128)S(1)} %get-tuple-element.423, s32[4096]{0:T(1024)S(1)} %get-tuple-element.379), kind=kCustom, calls=%fused_computation.2.clone.1 | custom fusion | bytes 49152 | tf_op jit(solution)/shard_map/while/body/gather | solution.py:12
  216.3 1.4 fusion.59
  217.7 0.7 fusion.60
  218.3 0.6 reshape.6
  219.0 0.0 all-reduce.7.cloned.1.call-update
  219.0 416.4 %all-reduce.7.cloned.1.call-done = f32[16,1024]{1,0:T(8,128)} async-done(((f32[16,1024]{1,0:T(8,128)}), f32[16,1024]{1,0:T(8,128)}) %all-reduce.7.cloned.1.call-update) | async-done | bytes 65552 | tf_op jit(solution)/shard_map/psum | solution.py:87
  635.4 1.5 copy.23
  (18 shorter events, 0.2 us)
Async XLA Ops:
  6.5 2.1 copy-start.4
  6.5 64.3 %all-reduce.9.cloned.1.call-start = ((), (), s32[]{:S(2)}) async-start(), calls=%async_computation.1 | async-start | bytes 2801664
  8.5 4.6 copy-start.7
  8.5 4.8 copy-start.8
  8.5 12.3 %copy-start.6 = (s32[256]{0:T(256)S(1)}, s32[256]{0:T(256)}, u32[]{:S(2)}) copy-start(s32[256]{0:T(256)} %param.19) | copy-start | bytes 3076
  8.5 22.6 %copy-start.5 = (s32[4096]{0:T(1024)S(1)}, s32[4096]{0:T(1024)}, u32[]{:S(2)}) copy-start(s32[4096]{0:T(1024)} %param.20) | copy-start | bytes 49156
  8.5 62.3 %copy-start.1 = (s32[12288]{0:T(1024)S(1)}, s32[12288]{0:T(1024)}, u32[]{:S(2)}) copy-start(s32[12288]{0:T(1024)} %param.12) | copy-start | bytes 147460
  8.5 62.3 %copy-start.2 = (s32[12288]{0:T(1024)S(1)}, s32[12288]{0:T(1024)}, u32[]{:S(2)}) copy-start(s32[12288]{0:T(1024)} %param.14) | copy-start | bytes 147460
  8.5 62.3 %copy-start.3 = (s32[12288]{0:T(1024)S(1)}, s32[12288]{0:T(1024)}, u32[]{:S(2)}) copy-start(s32[12288]{0:T(1024)} %param.13) | copy-start | bytes 147460
  9.9 1.1 copy-start
  11.0 624.3 %all-reduce.7.cloned.1.call-start = ((), (), s32[]{:S(2)}) async-start(), calls=%async_computation | async-start | bytes 131072 | tf_op jit(solution)/shard_map/psum | solution.py:87
Sparse Core Ops, SparseCore 0:
  11.2 59.5 all-reduce.8
  219.1 416.1 all-reduce.6
where the time goes:
time: 649 us; the launch traced here: 644 us
  waiting for transfers between devices  447 us (69%)
  local copies, waits for them, and re-layouts  152 us (23%)
  blocking collectives  26.6 us (4%)
  between operations  16.1 us (2%)
    psum x1, waiting for transfers between devices, shards(): result = lax.psum(group_sums, ('gx', 'gy'))  416 us
    gather x3, local copies, waits for them, and re-layouts, pick_bits(): chosen = packed[position // per_word]  73.6 us
    gather x1, local copies, waits for them, and re-layouts, add_block(): word_val = brand_table[brand_place(owner_idx, local_idx // 3)]  48.5 us
    unnamed x3, waiting for transfers between devices  30.8 us
    gather x1, local copies, waits for them, and re-layouts, add_block(): flag_word = product_bits[flag_place(owner_idx, local_idx // 32)]  23 us
  transfers between devices with their start and end apart: 2, of which 2 were waited for; matrix products, arithmetic and copies ran while one was open for 0% of the time, Pallas kernels for 0%

commit v1 on v0

--- a/solution.py
+++ b/solution.py
@@ -84,7 +84,7 @@
 
     totals = lax.fori_loop(0, block_total, add_block, jnp.zeros((high_groups, 128), jnp.float32))
     group_sums = totals.reshape(YEARS, BRANDS)
-    result = lax.psum(group_sums, ("gx", "gy"))
+    result = jnp.sum(lax.all_gather(group_sums, ("gx", "gy")), axis=0)
     return result
 
 

time: 649 us -> 587 us (0.904)
  waiting for transfers between devices: 447 us -> 383 us
    psum x1 -> x0, waiting for transfers between devices: 416 us -> none  [shards(): result = lax.psum(group_sums, ('gx', 'gy'))]
    all_gather x0 -> x1, waiting for transfers between devices: none -> 352 us  [shards(): result = jnp.sum(lax.all_gather(group_sums, ('gx', 'gy')), axis=0)]
where the time goes in v1:
time: 587 us; the launch traced here: 581 us
  waiting for transfers between devices  383 us (65%)
  local copies, waits for them, and re-layouts  151 us (26%)
  blocking collectives  26.6 us (5%)
  between operations  16 us (3%)
    all_gather x1, waiting for transfers between devices, shards(): result = jnp.sum(lax.all_gather(group_sums, ('gx', 'gy')), axis=0)  352 us
    gather x3, local copies, waits for them, and re-layouts, pick_bits(): chosen = packed[position // per_word]  73.6 us
    gather x1, local copies, waits for them, and re-layouts, add_block(): word_val = brand_table[brand_place(owner_idx, local_idx // 3)]  48.5 us
    unnamed x3, waiting for transfers between devices  30.8 us
    gather x1, local copies, waits for them, and re-layouts, add_block(): flag_word = product_bits[flag_place(owner_idx, local_idx // 32)]  23 us
  transfers between devices with their start and end apart: 2, of which 2 were waited for; matrix products, arithmetic and copies ran while one was open for 0% of the time, Pallas kernels for 0%

profile of v1, /device:TPU:1, one launch (start us, length us, event | category | flops | bytes accessed | tf_op | source)
XLA Modules:
  0.0 581.3 jit_solution(2953291015754119969)
XLA Ops:
  6.5 0.0 copy-start.3
  6.6 0.0 copy-start.2
  6.6 0.0 all-reduce.6.cloned.1.call-start
  6.6 1.3 dynamic-slice
  8.6 0.1 broadcast.223
  8.7 2.3 dynamic-update-slice.1
  11.0 0.0 copy-start
  11.0 1.1 copy-done
  12.1 0.0 all-reduce.6.cloned.1.call-update
  12.1 0.0 all-gather.3.cloned.1.call-start
  14.0 0.0 copy-done.6
  14.1 0.2 dynamic-update-slice
  14.3 0.2 dynamic-update-slice.2
  14.5 7.3 %all-reduce.3 = (s32[512]{0:T(512)S(1)}, s32[128]{0:T(128)S(1)}) all-reduce(s32[512]{0:T(512)S(1)} %dynamic-update-slice, s32[128]{0:T(128)S(1)} %dynamic-update-slice.2), channel_id=1, replica_groups=mesh['gx'=8,'gy'=4] {'gx'}, use_global_device_ids=true, to_apply=%add | all-reduce | flops 640 | bytes 5120
  21.8 0.0 copy-done.5
  21.8 10.3 %all-gather = s32[8,1,256]{2,1,0:T(1,128)S(1)} all-gather(s32[1,1,256]{2,1,0:T(1,128)S(1)} %bitcast.8), channel_id=1, replica_groups=mesh['gx'=8,'gy'=4] {'gx'}, dimensions={0}, use_global_device_ids=true | all-gather | bytes 9216 | tf_op jit(solution)/shard_map/all_gather | solution.py:35
  32.1 0.0 copy-done.4
  32.1 9.0 %all_gather.22 = s32[32768]{0:T(1024)S(1)} all-gather(s32[4096]{0:T(1024)S(1)} %copy-done.4), channel_id=1, replica_groups=mesh['gx'=8,'gy'=4] {'gx'}, dimensions={0}, use_global_device_ids=true | all-gather | bytes 147456 | tf_op jit(solution)/shard_map/all_gather | solution.py:36
  41.1 30.7 %all-reduce.6.cloned.1.call-done = s32[349568]{0:T(1024)} async-done(((s32[349568]{0:T(1024)}), s32[349568]{0:T(1024)}) %all-reduce.6.cloned.1.call-update) | async-done | bytes 1398288
  71.9 147.5 %while.13 = (s32[]{:T(128)}, f32[128,128]{1,0:T(8,128)S(1)}, s32[]{:T(128)}, s32[12288]{0:T(1024)S(1)}, s32[512]{0:T(512)S(1)}, /*index=5*/s32[12288]{0:T(1024)S...) while((s32[]{:T(128)}, f32[128,128]{1,0:T(8,128)S(1)}, ...), condition=%wide.region_1.2_spmd, body=%wide.region_0.1_spmd.sunk | while | flops 136749056 | bytes 860395 | solution.py:85
  72.0 48.5 %gather_fusion.1 = s32[4096]{0:T(1024)S(1)} fusion(s32[349568]{0:T(1024)} %get-tuple-element.421, s32[4096]{0:T(1024)S(1)} %fusion.57), kind=kCustom, calls=%fused_computation.1.clone.1 | custom fusion | bytes 49152 | tf_op jit(solution)/shard_map/while/body/gather | solution.py:68
  120.5 25.9 %gather_fusion = s32[4096]{0:T(1024)S(1)} fusion(s32[512]{0:T(512)S(1)} %get-tuple-element.419, s32[4096]{0:T(1024)S(1)} %fusion.55), kind=kCustom, calls=%fused_computation.clone.1 | custom fusion | bytes 49152 | tf_op jit(solution)/shard_map/while/body/gather | solution.py:12
  146.4 0.1 fusion.58
  146.5 23.0 %gather_fusion.3 = s32[4096]{0:T(1024)S(1)} fusion(s32[2048]{0:T(1024)S(1)} %get-tuple-element.425, s32[4096]{0:T(1024)S(1)} %get-tuple-element.378), kind=kCustom, calls=%fused_computation.3.clone.1 | custom fusion | bytes 49152 | tf_op jit(solution)/shard_map/while/body/gather | solution.py:12
  169.5 23.0 %gather_fusion.2 = s32[4096]{0:T(1024)S(1)} fusion(s32[32768]{0:T(1024)S(1)} %get-tuple-element.426, s32[4096]{0:T(1024)S(1)} %get-tuple-element.377), kind=kCustom, calls=%fused_computation.4.clone.1 | custom fusion | bytes 49152 | tf_op jit(solution)/shard_map/while/body/gather | solution.py:61
  192.6 24.7 %gather_fusion.4 = s32[4096]{0:T(1024)S(1)} fusion(s32[128]{0:T(128)S(1)} %get-tuple-element.423, s32[4096]{0:T(1024)S(1)} %get-tuple-element.379), kind=kCustom, calls=%fused_computation.2.clone.1 | custom fusion | bytes 49152 | tf_op jit(solution)/shard_map/while/body/gather | solution.py:12
  217.3 1.4 fusion.59
  218.7 0.7 fusion.60
  219.4 0.6 all_gather_reshape.3
  220.0 0.0 all-gather.3.cloned.1.call-update
  220.0 352.1 %all-gather.3.cloned.1.call-done = f32[32,16,1024]{2,1,0:T(8,128)} async-done(((f32[1,16,1024]{2,1,0:T(8,128)}), f32[32,16,1024]{2,1,0:T(8,128)}) %all-gather.3.cloned.1.call-update) | async-done | bytes 2097168 | tf_op jit(solution)/shard_map/all_gather | solution.py:87
  572.1 2.3 reduce_sum.9
  (16 shorter events, 0.2 us)
Async XLA Ops:
  6.5 7.5 %copy-start.6 = (s32[64]{0:T(128)S(1)}, s32[64]{0:T(128)}, u32[]{:S(2)}) copy-start(s32[64]{0:T(128)} %param.17) | copy-start | bytes 772
  6.5 7.8 %copy-start.7 = (s32[16]{0:T(128)S(1)}, s32[16]{0:T(128)}, u32[]{:S(2)}) copy-start(s32[16]{0:T(128)} %param.18) | copy-start | bytes 196
  6.5 15.3 %copy-start.5 = (s32[256]{0:T(256)S(1)}, s32[256]{0:T(256)}, u32[]{:S(2)}) copy-start(s32[256]{0:T(256)} %param.19) | copy-start | bytes 3076
  6.5 25.6 %copy-start.4 = (s32[4096]{0:T(1024)S(1)}, s32[4096]{0:T(1024)}, u32[]{:S(2)}) copy-start(s32[4096]{0:T(1024)} %param.20) | copy-start | bytes 49156
  6.5 65.3 %copy-start.1 = (s32[12288]{0:T(1024)S(1)}, s32[12288]{0:T(1024)}, u32[]{:S(2)}) copy-start(s32[12288]{0:T(1024)} %param.12) | copy-start | bytes 147460
  6.5 65.3 %copy-start.3 = (s32[12288]{0:T(1024)S(1)}, s32[12288]{0:T(1024)}, u32[]{:S(2)}) copy-start(s32[12288]{0:T(1024)} %param.13) | copy-start | bytes 147460
  6.6 65.3 %copy-start.2 = (s32[12288]{0:T(1024)S(1)}, s32[12288]{0:T(1024)}, u32[]{:S(2)}) copy-start(s32[12288]{0:T(1024)} %param.14) | copy-start | bytes 147460
  6.6 65.3 %all-reduce.6.cloned.1.call-start = ((), (), s32[]{:S(2)}) async-start(), calls=%async_computation.1 | async-start | bytes 2801664
  11.0 1.1 copy-start
  12.1 560.1 %all-gather.3.cloned.1.call-start = ((), (), s32[]{:S(2)}) async-start(), calls=%async_computation | async-start | bytes 2162688 | tf_op jit(solution)/shard_map/all_gather | solution.py:87
Sparse Core Ops, SparseCore 0:
  12.2 59.5 all-reduce.5
  220.2 351.9 all-gather.2
